TPU v7x, 128 devices: a whole 4x4x4 slice. The times are simulated.
128 devices in a mesh: grp: 8 (over y, core), mem: 16 (over x, z).
Axes of the slice: x: 4, y: 4, z: 4, core: 2. Of those that a mesh axis runs over, the one named last changes fastest.
Arguments:
- factors: bfloat16 [256, 288, 1792], P(('grp', 'mem')), may hold values from -3 to 3
- screen: int32 [128, 18], P(('grp', 'mem')), may hold values from 0 to 1, as said below
Outputs:
- exchange_matrix: float32 [1792, 1792], P(('grp', 'mem'))
Inputs may be any that keep to these rules, and one draw needn't show every extreme that they name: screen[b, j] is 1 where auxiliary block b and occupied block j survive screening; every auxiliary block keeps at least one occupied block.
All inputs are finite; a program needn't handle non-finite values.
Results may differ from a plain program's by a relative error of at most 0.0003.
Values may be sent and summed in bfloat16 or wider, within the bound.
A program may use at most 128 MiB of HBM per device.

v0:
```python
import jax
import jax.numpy as jnp
from jax import lax
from jax.sharding import PartitionSpec as P


def split_up(x, dim, size):
    before, after = (x.shape[:dim], x.shape[dim + 1 :])
    return jnp.moveaxis(x.reshape(*before, size, -1, *after), dim, 0)


def sent_and_summed(x, axis, dim):
    blocks = split_up(x, dim, lax.axis_size(axis))
    arrived = lax.all_to_all(blocks, axis, split_axis=0, concat_axis=0, tiled=True)
    return arrived.sum(axis=0)


def on_device(factors, screen):
    aux_rows, occ_count, basis = factors.shape
    occ_blocks = screen.shape[1]
    occ_width = occ_count // occ_blocks
    blocks = factors.reshape(aux_rows, occ_blocks, occ_width, basis)
    kept_flag = screen[0]
    active = kept_flag == 1
    per_turn = max(1, 512 // (aux_rows * occ_width))
    active_int = active.astype(jnp.int32)
    block_order = jnp.argsort(1 - active_int, stable=True)
    block_order = jnp.concatenate([block_order, jnp.zeros((per_turn,), jnp.int32)])
    live_count = jnp.sum(active_int)
    turn_count = (live_count + per_turn - 1) // per_turn
    turn_slots = jnp.arange(per_turn, dtype=jnp.int32)
    groups = lax.axis_size("grp")
    members_all = lax.axis_size("mem")
    own_rows = basis // (groups * members_all)

    def add_turn(turn, running):
        picked = lax.dynamic_slice_in_dim(block_order, turn * per_turn, per_turn)
        weight = (turn * per_turn + turn_slots < live_count).astype(jnp.bfloat16)
        chosen = jnp.take(blocks, picked, axis=1) * weight[None, :, None, None]
        flat_rows = chosen.reshape(-1, basis)
        return running + lax.dot_general(
            flat_rows, flat_rows, (((0,), (0,)), ((), ())), preferred_element_type=jnp.float32
        )

    whole = lax.fori_loop(0, turn_count, add_turn, jnp.zeros((basis, basis), jnp.float32))
    sectioned = whole.reshape(groups, members_all, own_rows, basis)
    member_sum = lax.psum_scatter(sectioned, "mem", scatter_dimension=1, tiled=True)
    group_sum = sent_and_summed(member_sum, "grp", 0)
    result_rows = group_sum.reshape(own_rows, basis)
    return result_rows


def solution(mesh):
    placed = (P(("grp", "mem"), None, None), P(("grp", "mem"), None))
    return jax.shard_map(
        on_device, mesh=mesh, in_specs=placed, out_specs=P(("grp", "mem"), None), check_vma=False
    )
```

profile of v0, /device:TPU:1, one launch (start us, length us, event | category | flops | bytes accessed | tf_op | source)
XLA Modules:
  0.0 201.0 jit_solution(172686779110996353)
XLA Ops:
  6.5 0.0 reduce-scatter.4.cloned.1.call-start
  6.5 1.4 subtract_bitcast_fusion
  8.6 1.6 sort.17
  10.2 5.5 %broadcast_in_dim.16 = f32[1792,1792]{1,0:T(8,128)} broadcast(f32[]{:T(128)} %constant.43.clone.1), dimensions={} | broadcast | bytes 12845060 | tf_op jit(solution)/shard_map/broadcast_in_dim | solution.py:45
  15.8 12.7 %while.11 = (s32[]{:T(128)}, f32[1792,1792]{1,0:T(8,128)}, s32[]{:T(128)}, s32[34]{0:T(128)S(1)}, bf16[2,18,16,1792]{3,2,1,0:T(8,128)(2,1)}, /*index=5*/s32[]{:T(128)}, s32[]{:T(128)}, s32[]{:T(128)}, s32[]{:T(128)}, s32[]{:T(128)}) while((s32[]{:T(128)}, f32[1792,1792]{1,0:T(8,128)}, s32[]{:T(128)}, s32[34]{0:T(128)S(1)}, ...), condition=%wide.region_3.4_spmd.clone, body=%wide.region_2.3_spmd.clone.sunk | while | flops 3293381888 | bytes 31199744 | solution.py:45
  15.8 0.8 compare_and_fusion.2
  16.5 2.2 %gather_fusion = bf16[16,2,16,1792]{3,2,1,0:T(8,128)(2,1)S(1)} fusion(bf16[2,18,16,1792]{3,2,1,0:T(8,128)(2,1)} %get-tuple-element.146, s32[1024]{0:T(1024)S(1)} %pad_clamp_fusion.2), kind=kCustom, calls=%fused_computation.clone.clone.1 | custom fusion | bytes 3670080 | tf_op jit(solution)/shard_map/while/body/jit(_take)/gather | solution.py:39
  18.8 9.7 %bitcast_add_fusion.2 = f32[1792,1792]{1,0:T(8,128)} fusion(f32[1792,1792]{1,0:T(8,128)} %get-tuple-element.133, bf16[16,2,16,1792]{3,2,1,0:T(8,128)(2,1)S(1)} %gather_fusion, pred[16]{0:T(512)(128)(4,1)S(1)} %get-tuple-element.120, bf16[16]{0:T(256)(128)(2,1)S(1)} %get-tuple-element.121), kind=kOutput, calls=%fused_computation.2.clone.1 | convolution fusion | flops 3293380608 | bytes 27525168 | tf_op jit(solution)/shard_map/while/body/dot_general | solution.py:41
  28.5 13.9 %reshape.29 = f32[8,16,14,1792]{3,2,1,0:T(8,128)} reshape(f32[1792,1792]{1,0:T(8,128)} %get-tuple-element.45) | data formatting | bytes 25690112 | tf_op jit(solution)/shard_map/reshape | solution.py:46
  42.4 19.8 %copy.9 = f32[8,16,14,1792]{3,0,2,1:T(8,128)} copy(f32[8,16,14,1792]{3,2,1,0:T(8,128)} %reshape.29) | data formatting | bytes 25690112 | tf_op jit(solution)/shard_map/reshape | solution.py:46
  62.2 0.0 reduce-scatter.4.cloned.1.call-update
  62.2 110.6 %reduce-scatter.4.cloned.1.call-done = f32[8,1,14,1792]{3,0,2,1:T(8,128)} async-done(((f32[8,16,14,1792]{3,0,2,1:T(8,128)}), f32[8,1,14,1792]{3,0,2,1:T(8,128)}) %reduce-scatter.4.cloned.1.call-update) | async-done | bytes 802832
  172.8 2.0 copy.10
  174.7 18.1 %all_to_all.5 = f32[8,1,1,14,1792]{4,2,3,1,0:T(1,128)S(1)} all-to-all(f32[8,1,1,14,1792]{4,2,3,1,0:T(1,128)S(1)} %copy.10), channel_id=1, replica_groups=mesh['grp'=8,'mem'=16] {'grp'}, dimensions={0} | all-to-all | bytes 1605632 | tf_op jit(solution)/shard_map/all_to_all | solution.py:14
  192.8 1.3 reduce_sum.19
  (3 shorter events, 0.0 us)
Async XLA Ops:
  6.5 166.2 %reduce-scatter.4.cloned.1.call-start = ((), (), s32[]{:S(2)}) async-start(), calls=%async_computation.2 | async-start | bytes 13647872
Sparse Core Ops, SparseCore 0:
  62.3 110.4 reduce-scatter.3
where the time goes:
time: 202 us; the launch traced here: 201 us
  waiting for transfers between devices  111 us (55%)
  local copies, waits for them, and re-layouts  43.4 us (21%)
  blocking collectives  18.1 us (9%)
  between operations  14.1 us (7%)
  matrix products  9.72 us (5%)
  other arithmetic  5.09 us (3%)
    unnamed x2, waiting for transfers between devices  111 us
    reshape x2, local copies, waits for them, and re-layouts, on_device(): sectioned = whole.reshape(groups, members_all, own_rows, basis)  33.7 us
    all_to_all x1, blocking collectives, sent_and_summed(): lax.all_to_all(blocks, axis, split_axis=0, concat_axis=0, tiled=True)  18.1 us
    dot_general x1, matrix products, add_turn(): lax.dot_general(flat_rows, flat_rows, (((0,), (0,)), ((), ())), preferred...  9.72 us
    broadcast_in_dim x1, local copies, waits for them, and re-layouts, on_device(): jnp.zeros((basis, basis), jnp.float32)  5.51 us
  transfers between devices with their start and end apart: 1, of which 1 were waited for; matrix products, arithmetic and copies ran while one was open for 0% of the time, Pallas kernels for 0%

commit v1 on v0

v1 whole, which is shorter than its diff:
```python
import jax
import jax.numpy as jnp
from jax import lax
from jax.experimental import pallas as pl
from jax.experimental.pallas import tpu as pltpu
from jax.sharding import PartitionSpec as P

MESH = pl.DeviceIdType.MESH
NBF = 1792
ROWS = 576
DEPTH = 640
TOP = 32000.0
X, Y, Z = 0, 1, 2
COLOURS = (
    ((X, Y, Z), 0, 640, 56, 14),
    ((Y, Z, X), 640, 640, 56, 14),
    ((Z, X, Y), 1280, 512, 64, 16),
)
HOPS = (1, 3, 2)


def encoded(value, inverse):
    level = lax.rsqrt(lax.rsqrt(jnp.abs(value) * inverse)) * TOP + 0.5
    code = level.astype(jnp.int32)
    return jnp.where(value < 0.0, -code, code).astype(jnp.int16)


def decoded(code, scale):
    level = code.astype(jnp.int32).astype(jnp.float32)
    return level * jnp.abs(level) * (level * level) * scale


def kernel(
    f_ref, s_ref, o_ref,
    fbuf, pick, t1, ft0, ft1, ft2, whole,
    q10, q11, q12, r10, r11, r12, a0, a1, a2,
    q20, q21, q22, r20, r21, r22,
    b0, b1, b2, q30, q31, q32, r30, r31, r32,
    peer_screen, sc_own, sc_peer, sc1, sc2s, sc2, sc3s, sc3,
    load_sem, swap_send, swap_recv, send1, recv1, send2, recv2, send3, recv3,
    ssend1, srecv1, ssend2, srecv2, ssend3, srecv3,
):
    grp, mem = lax.axis_index("grp"), lax.axis_index("mem")
    here = (mem // 4, grp // 2, mem % 4)
    core = grp % 2

    def along(axis, hop):
        at = list(here)
        at[axis] = (at[axis] + hop) % 4
        return (at[Y] * 2 + core, at[X] * 4 + at[Z])

    peer = (here[Y] * 2 + 1 - core, mem)

    loads = [
        pltpu.make_async_copy(f_ref.at[i], fbuf.at[pl.ds(i * 288, 288)], load_sem.at[i])
        for i in range(2)
    ]
    for load in loads:
        load.start()

    barrier = pltpu.get_barrier_semaphore()
    pl.semaphore_signal(barrier, inc=1, device_id=peer, device_id_type=MESH)
    for axis in range(3):
        for hop in HOPS:
            pl.semaphore_signal(barrier, inc=1, device_id=along(axis, hop), device_id_type=MESH)

    def where_from(rows, first, kind):
        r = lax.broadcasted_iota(jnp.int32, (rows, 384), 0).astype(jnp.float32)
        l = lax.broadcasted_iota(jnp.int32, (rows, 384), 1).astype(jnp.float32)
        if kind == 0:
            n = r
        else:
            w = 14.0 if kind == 1 else 16.0
            z = jnp.floor((r + 0.5) * (1.0 / (4 * w)))
            x = jnp.floor((r - z * (4 * w) + 0.5) * (1.0 / w))
            i = r - z * (4 * w) - x * w
            n = jnp.where(i < 14.0, x * 56.0 + z * 14.0 + i, 4096.0)
        pick[pl.ds(first, rows), :] = l - n

    where_from(224, 0, 0)
    where_from(224, 224, 1)
    where_from(256, 448, 2)
    zero_rows = jnp.zeros((DEPTH - ROWS, NBF), jnp.bfloat16)
    fbuf[pl.ds(ROWS, DEPTH - ROWS), :] = zero_rows
    fbuf[pl.ds(DEPTH + ROWS, DEPTH - ROWS), :] = zero_rows

    pl.semaphore_wait(barrier, 10)
    swaps = [
        pltpu.make_async_remote_copy(
            src_ref=f_ref.at[i], dst_ref=fbuf.at[pl.ds(DEPTH + i * 288, 288)],
            send_sem=swap_send.at[i], recv_sem=swap_recv.at[i], device_id=peer, device_id_type=MESH,
        )
        for i in range(2)
    ]
    swaps.append(
        pltpu.make_async_remote_copy(
            src_ref=s_ref, dst_ref=peer_screen, send_sem=swap_send.at[2], recv_sem=swap_recv.at[2],
            device_id=peer, device_id_type=MESH,
        )
    )
    for swap in swaps:
        swap.start()

    k = lax.broadcasted_iota(jnp.int32, (18, DEPTH), 1)
    j = lax.broadcasted_iota(jnp.int32, (18, DEPTH), 0) * 16
    k = jnp.where(k >= 288, k - 288, k)
    spread = jnp.where((k >= j) & (k < j + 16), 1.0, 0.0).astype(jnp.bfloat16)

    def mask_of(ref):
        kept = jnp.where(ref[...] == 1, 1.0, 0.0).astype(jnp.bfloat16)
        kept = jnp.broadcast_to(kept, (16, 18))
        m = jnp.dot(kept, spread, preferred_element_type=jnp.float32)
        lane = lax.broadcasted_iota(jnp.int32, (16, DEPTH), 1)
        return jnp.where(lane < ROWS, m, 0.0)

    def prepare(first, mask):
        def one(y, _):
            g = 2 * y + core
            tile = (224 * g) // 128 - g // 7
            off = 224 * g - 128 * tile
            window = fbuf[pl.ds(first, DEPTH), pl.ds(pl.multiple_of(tile * 128, 128), 384)]
            offset = off.astype(jnp.float32)

            def taken(at, rows):
                chosen = jnp.where(pick[pl.ds(at, rows), :] == offset, 1.0, 0.0).astype(jnp.bfloat16)
                got = lax.dot_general(
                    chosen, window, (((1,), (1,)), ((), ())), preferred_element_type=jnp.float32
                )
                return got * mask[0:1]

            columns = pl.ds(first, DEPTH)
            ft0[y, :, columns] = taken(0, 224).astype(jnp.bfloat16)
            got = taken(224, 224)
            for z in range(4):
                t1[z, y] = got[z * 56 : z * 56 + 56]
            got = taken(448, 256).astype(jnp.bfloat16)
            for z in range(4):
                for x in range(4):
                    at = (z * 4 + x) * 16
                    ft2[x, z, y, :, columns] = got[at : at + 16]
            return 0

        lax.fori_loop(0, 4, one, 0)
        for z in range(4):
            ft1[z, :, pl.ds(first, DEPTH)] = t1[z].reshape(224, DEPTH).astype(jnp.bfloat16)

    for load in loads:
        load.wait()
    own_mask = mask_of(s_ref)
    own = fbuf[pl.ds(0, DEPTH), :]
    squares = jnp.dot(own_mask.astype(jnp.bfloat16), own * own, preferred_element_type=jnp.float32)
    most = jnp.max(squares[0:8], axis=1, keepdims=True) * 1.02 + 1e-30
    sc_own[...] = jnp.broadcast_to(most, (8, 128))
    scale_swap = pltpu.make_async_remote_copy(
        src_ref=sc_own, dst_ref=sc_peer, send_sem=swap_send.at[3], recv_sem=swap_recv.at[3],
        device_id=peer, device_id_type=MESH,
    )
    scale_swap.start()
    swaps.append(scale_swap)
    prepare(0, own_mask)
    scale_swap.wait_recv()
    mine = sc_own[...] + sc_peer[...]

    sent = []
    sc1[9] = mine
    for axis in range(3):
        for hop in HOPS:
            copy = pltpu.make_async_remote_copy(
                src_ref=sc1.at[9], dst_ref=sc1.at[axis * 3 + hop - 1],
                send_sem=ssend1.at[axis * 3 + hop - 1], recv_sem=srecv1.at[axis * 3 + hop - 1],
                device_id=along(axis, hop), device_id_type=MESH,
            )
            copy.start()
            sent.append(copy)
    scale_copies1 = list(sent)

    for swap in swaps[:3]:
        swap.wait_recv()
    prepare(DEPTH, mask_of(peer_screen))

    q1, r1, a = (q10, q11, q12), (r10, r11, r12), (a0, a1, a2)
    q2, r2, b = (q20, q21, q22), (r20, r21, r22), (b0, b1, b2)
    q3, r3 = (q30, q31, q32), (r30, r31, r32)
    inverse = (1.0 / mine)[0:1, 0:1]

    first_copies = {}
    for step, hop2 in enumerate((1, 3, 2, 0)):
        for c, (axes, col, cols, rows, _) in enumerate(COLOURS):
            v = (here[axes[1]] + hop2) % 4
            lhs = ft0[v] if c == 0 else ft1[v] if c == 1 else ft2[v].reshape(256, 2 * DEPTH)
            made = jnp.dot(lhs, fbuf[:, pl.ds(col, cols)], preferred_element_type=jnp.float32)
            whole[:, pl.ds(0, rows), pl.ds(0, cols)] = made.reshape(4, rows, cols)
            for hop in HOPS:
                u = (here[axes[0]] + hop) % 4
                q1[c][hop - 1, step] = encoded(whole[u, pl.ds(0, rows), pl.ds(0, cols)], inverse)
                copy = pltpu.make_async_remote_copy(
                    src_ref=q1[c].at[hop - 1, step], dst_ref=r1[c].at[hop - 1, step],
                    send_sem=send1.at[c, hop - 1, step], recv_sem=recv1.at[c, hop - 1, step],
                    device_id=along(axes[0], hop), device_id_type=MESH,
                )
                copy.start()
                sent.append(copy)
                first_copies[c, hop, step] = copy
            a[c][step] = whole[here[axes[0]], pl.ds(0, rows), pl.ds(0, cols)]

    for copy in scale_copies1:
        copy.wait_recv()
    unit = 1.0 / (TOP * TOP) / (TOP * TOP)
    scale2_copies = []
    for c, (axes, *_) in enumerate(COLOURS):
        at = axes[0] * 3
        sc2s[c] = mine + sc1[at] + sc1[at + 1] + sc1[at + 2]
        for hop in HOPS:
            copy = pltpu.make_async_remote_copy(
                src_ref=sc2s.at[c], dst_ref=sc2.at[c, hop - 1],
                send_sem=ssend2.at[c, hop - 1], recv_sem=srecv2.at[c, hop - 1],
                device_id=along(axes[1], hop), device_id_type=MESH,
            )
            copy.start()
            sent.append(copy)
            scale2_copies.append(copy)

    second_copies = {}

    def summed1(c, step):
        axes = COLOURS[c][0]
        total = a[c][step]
        for hop in HOPS:
            first_copies[c, hop, step].wait_recv()
            scale = sc1[axes[0] * 3 + hop - 1][0:1, 0:1] * unit
            total = total + decoded(r1[c][hop - 1, step], scale)
        return total

    for step, hop2 in enumerate(HOPS):
        for c, (axes, *_) in enumerate(COLOURS):
            inv2 = (1.0 / sc2s[c])[0:1, 0:1]
            q2[c][hop2 - 1] = encoded(summed1(c, step), inv2)
            copy = pltpu.make_async_remote_copy(
                src_ref=q2[c].at[hop2 - 1], dst_ref=r2[c].at[hop2 - 1],
                send_sem=send2.at[c, hop2 - 1], recv_sem=recv2.at[c, hop2 - 1],
                device_id=along(axes[1], hop2), device_id_type=MESH,
            )
            copy.start()
            sent.append(copy)
            second_copies[c, hop2] = copy

    for copy in scale2_copies:
        copy.wait_recv()
    scale3_copies = []
    for c, (axes, *_) in enumerate(COLOURS):
        sc3s[c] = sc2s[c] + sc2[c, 0] + sc2[c, 1] + sc2[c, 2]
        for hop in HOPS:
            copy = pltpu.make_async_remote_copy(
                src_ref=sc3s.at[c], dst_ref=sc3.at[c, hop - 1],
                send_sem=ssend3.at[c, hop - 1], recv_sem=srecv3.at[c, hop - 1],
                device_id=along(axes[2], hop), device_id_type=MESH,
            )
            copy.start()
            sent.append(copy)
            scale3_copies.append(copy)

    for c in range(3):
        a[c][3] = summed1(c, 3)

    third_copies = {}
    for c, (axes, _, cols, rows, own_rows) in enumerate(COLOURS):
        total = a[c][3]
        for hop in HOPS:
            second_copies[c, hop].wait_recv()
            total = total + decoded(r2[c][hop - 1], sc2[c, hop - 1][0:1, 0:1] * unit)
        for w in range(4):
            b[c][w, pl.ds(0, own_rows), :] = total[w * own_rows : (w + 1) * own_rows]
        inv3 = (1.0 / sc3s[c])[0:1, 0:1]
        for hop in HOPS:
            w = (here[axes[2]] + hop) % 4
            q3[c][hop - 1, pl.ds(0, own_rows), :] = encoded(b[c][w, pl.ds(0, own_rows), :], inv3)
            copy = pltpu.make_async_remote_copy(
                src_ref=q3[c].at[hop - 1], dst_ref=r3[c].at[hop - 1],
                send_sem=send3.at[c, hop - 1], recv_sem=recv3.at[c, hop - 1],
                device_id=along(axes[2], hop), device_id_type=MESH,
            )
            copy.start()
            sent.append(copy)
            third_copies[c, hop] = copy

    for copy in scale3_copies:
        copy.wait_recv()
    for c, (axes, col, cols, _, _) in enumerate(COLOURS):
        total = b[c][here[axes[2]], pl.ds(0, 14), :]
        for hop in HOPS:
            third_copies[c, hop].wait_recv()
            scale = sc3[c, hop - 1][0:1, 0:1] * unit
            total = total + decoded(r3[c][hop - 1, pl.ds(0, 14), :], scale)
        o_ref[:, pl.ds(col, cols)] = total

    for copy in swaps + sent:
        copy.wait_send()


def on_device(factors, screen):
    f32, i16, bf16 = jnp.float32, jnp.int16, jnp.bfloat16
    v = pltpu.VMEM
    dma = pltpu.SemaphoreType.DMA
    per = [(c[2], c[3]) for c in COLOURS]
    scratch = [
        v((2 * DEPTH, NBF), bf16), v((704, 384), f32), v((4, 4, 56, DEPTH), f32),
        v((4, 224, 2 * DEPTH), bf16), v((4, 224, 2 * DEPTH), bf16), v((4, 4, 4, 16, 2 * DEPTH), bf16),
        v((4, 64, 640), f32),
        *[v((3, 4, rows, cols), i16) for cols, rows in per],
        *[v((3, 4, rows, cols), i16) for cols, rows in per],
        *[v((4, rows, cols), f32) for cols, rows in per],
        *[v((3, rows, cols), i16) for cols, rows in per],
        *[v((3, rows, cols), i16) for cols, rows in per],
        *[v((4, 16, cols), f32) for cols, rows in per],
        *[v((3, 16, cols), i16) for cols, rows in per],
        *[v((3, 16, cols), i16) for cols, rows in per],
        v((1, 18), jnp.int32), v((8, 128), f32), v((8, 128), f32), v((10, 8, 128), f32),
        v((3, 8, 128), f32), v((3, 3, 8, 128), f32), v((3, 8, 128), f32), v((3, 3, 8, 128), f32),
        dma((2,)), dma((4,)), dma((4,)), dma((3, 3, 4)), dma((3, 3, 4)), dma((3, 3)), dma((3, 3)),
        dma((3, 3)), dma((3, 3)), dma((9,)), dma((9,)), dma((3, 3)), dma((3, 3)), dma((3, 3)), dma((3, 3)),
    ]
    return pl.pallas_call(
        kernel,
        out_shape=jax.ShapeDtypeStruct((14, NBF), f32),
        in_specs=[pl.BlockSpec(memory_space=pl.ANY), pl.BlockSpec(memory_space=pltpu.VMEM)],
        out_specs=pl.BlockSpec(memory_space=pltpu.VMEM),
        scratch_shapes=scratch,
        compiler_params=pltpu.CompilerParams(
            collective_id=0, has_side_effects=True, vmem_limit_bytes=60 * 2**20
        ),
    )(factors, screen)


def solution(mesh):
    placed = (P(("grp", "mem"), None, None), P(("grp", "mem"), None))
    return jax.shard_map(
        on_device, mesh=mesh, in_specs=placed, out_specs=P(("grp", "mem"), None), check_vma=False
    )
```

time: 202 us -> 43.4 us (0.21)
  waiting for transfers between devices: 111 us -> 0 us
  local copies, waits for them, and re-layouts: 43.4 us -> 1.55 us
  Pallas kernels: 0 us -> 41.3 us
  blocking collectives: 18.1 us -> 0 us
  between operations: 14.1 us -> 0.01 us
  matrix products: 9.72 us -> 0 us
  other arithmetic: 5.09 us -> 0 us
    unnamed x2 -> x0, waiting for transfers between devices: 111 us -> none
    pallas_call x0 -> x1, Pallas kernels: none -> 41.3 us  [on_device(): pl.pallas_call(kernel, out_shape=jax.ShapeDtypeStruct((14, NBF), f32), in...]
    reshape x3 -> x0, local copies, waits for them, and re-layouts: 35.6 us -> none  [the longest x2 33.7 us: on_device(): sectioned = whole.reshape(groups, members_all, own_rows, basis)]
    all_to_all x1 -> x0, blocking collectives: 18.1 us -> none  [sent_and_summed(): lax.all_to_all(blocks, axis, split_axis=0, concat_axis=0, tiled=True)]
    dot_general x1 -> x0, matrix products: 9.72 us -> none  [add_turn(): lax.dot_general(flat_rows, flat_rows, (((0,), (0,)), ((), ())), preferred...]
    broadcast_in_dim x1 -> x0, local copies, waits for them, and re-layouts: 5.51 us -> none  [on_device(): jnp.zeros((basis, basis), jnp.float32)]
    gather x1 -> x0, local copies, waits for them, and re-layouts: 2.25 us -> none  [add_turn(): chosen = jnp.take(blocks, picked, axis=1) * weight[None, :, None, None]]
  transfers between devices with their start and end apart: 1 -> 0, of which waited for: 1 -> 0; matrix products, arithmetic and copies ran while one was open for 0% -> 0% of each run, Pallas kernels for 0% -> 0%
where the time goes in v1:
time: 43.4 us; the launch traced here: 42.9 us
  Pallas kernels  41.3 us (95%)
  local copies, waits for them, and re-layouts  1.55 us (4%)
    pallas_call x1, Pallas kernels, on_device(): pl.pallas_call(kernel, out_shape=jax.ShapeDtypeStruct((14, NBF), f32), in...  41.3 us
    unnamed x1, local copies, waits for them, and re-layouts  1.55 us

profile of v1, /device:TPU:1, one launch (start us, length us, event | category | flops | bytes accessed | tf_op | source)
XLA Modules:
  0.0 42.9 jit_solution(9529084208851478680)
XLA Ops:
  0.0 41.3 %shard_map.28 = f32[14,1792]{1,0:T(8,128)} custom-call(bf16[2,288,1792]{2,1,0:T(8,128)(2,1)} %f_ref.1, s32[1,18]{1,0:T(1,128)} %s_ref.1), custom_call_target="tpu_custom_call" | custom-call | tf_op jit(solution)/shard_map/pallas_call | solution.py:322
  41.3 1.6 %copy.4 = f32[14,1792]{1,0:T(8,128)} copy(f32[14,1792]{1,0:T(8,128)} %shard_map.28) | data formatting | bytes 200704

commit v2 on v0

v2 whole, which is shorter than its diff:
```python
import jax
import jax.numpy as jnp
from jax import lax
from jax.experimental import pallas as pl
from jax.experimental.pallas import tpu as pltpu
from jax.sharding import PartitionSpec as P

MESH = pl.DeviceIdType.MESH
NBF = 1792
ROWS = 576
DEPTH = 640
CHUNK = 256
TOP = 32000.0
X, Y, Z = 0, 1, 2
COLOURS = (((X, Y, Z), 0, 640), ((Y, X, Z), 1280, 512), ((Z, Y, X), 640, 640))
HOPS = (1, 3, 2)
ALL = (1, 3, 2, 0)


def coded(value, inverse):
    level = lax.rsqrt(lax.rsqrt(jnp.abs(value) * inverse)) * TOP + 0.5
    code = level.astype(jnp.int32)
    return jnp.where(value < 0.0, -code, code)


def decoded(code, scale):
    level = code.astype(jnp.int32).astype(jnp.float32) * (1.0 / TOP)
    return level * jnp.abs(level) * (level * level) * scale


def power(exponent):
    return jnp.exp2(exponent)


def kernel(
    f_ref, s_ref, o_ref,
    fbuf, turned, order, g_rows, p_rows, w00, w01, w02, w03, w1, w20, w21, w22, w23,
    q10, q11, q12, r10, r11, r12,
    q20, q21, q22, r20, r21, r22, b0, b1, b2,
    own_screen, peer_screen, sc_own, sc_peer, mine_ref, sc1, exponents,
    load_sem, swap_send, swap_recv, send1, recv1, send2, recv2, ssend1, srecv1,
):
    q1, r1 = (q10, q11, q12), (r10, r11, r12)
    whole = ((w00, w01, w02, w03), w1, (w20, w21, w22, w23))
    q2, r2, b = (q20, q21, q22), (r20, r21, r22), (b0, b1, b2)
    grp, mem = lax.axis_index("grp"), lax.axis_index("mem")
    here = (mem // 4, grp // 2, mem % 4)
    core = grp % 2

    def at(axis, coordinate):
        place = list(here)
        place[axis] = coordinate
        return (place[Y] * 2 + core, place[X] * 4 + place[Z])

    def along(axis, hop):
        return at(axis, (here[axis] + hop) % 4)

    def remote(src, dst, send, recv, device):
        copy = pltpu.make_async_remote_copy(
            src_ref=src, dst_ref=dst, send_sem=send, recv_sem=recv, device_id=device, device_id_type=MESH
        )
        copy.start()
        sent.append(copy)
        return copy

    sent = []
    peer = (here[Y] * 2 + 1 - core, mem)
    barrier = pltpu.get_barrier_semaphore()
    pl.semaphore_signal(barrier, inc=1, device_id=peer, device_id_type=MESH)
    for axis in range(3):
        for hop in HOPS:
            pl.semaphore_signal(barrier, inc=1, device_id=along(axis, hop), device_id_type=MESH)
    loads = [
        pltpu.make_async_copy(f_ref.at[pl.ds(i * 144, 144)], fbuf.at[pl.ds(i * 144, 144)], load_sem.at[i])
        for i in range(4)
    ]
    loads.append(pltpu.make_async_copy(s_ref, own_screen, load_sem.at[4]))
    for load in loads:
        load.start()

    pl.semaphore_wait(barrier, 10)
    screen_swap = remote(s_ref, peer_screen, swap_send.at[7], swap_recv.at[7], peer)
    swaps = []

    def swap(i):
        columns = pl.ds(i * CHUNK, CHUNK)
        swaps.append(
            remote(
                fbuf.at[pl.ds(0, ROWS), columns],
                fbuf.at[pl.ds(DEPTH, ROWS), columns],
                swap_send.at[i], swap_recv.at[i], peer,
            )
        )

    for load in loads[:4]:
        load.wait()
    for i in range(4):
        swap(i)

    r = lax.broadcasted_iota(jnp.int32, (224, 224), 0).astype(jnp.float32)
    n = lax.broadcasted_iota(jnp.int32, (224, 224), 1).astype(jnp.float32)
    z = jnp.floor((r + 0.5) * (1.0 / 56.0))
    x = jnp.floor((r - z * 56.0 + 0.5) * (1.0 / 14.0))
    order[...] = jnp.where(r - z * 42.0 + x * 42.0 == n, 1.0, 0.0).astype(jnp.bfloat16)
    zero_rows = jnp.zeros((DEPTH - ROWS, NBF), jnp.bfloat16)
    fbuf[pl.ds(ROWS, DEPTH - ROWS), :] = zero_rows
    fbuf[pl.ds(DEPTH + ROWS, DEPTH - ROWS), :] = zero_rows
    kk = lax.broadcasted_iota(jnp.int32, (18, DEPTH), 1)
    jj = lax.broadcasted_iota(jnp.int32, (18, DEPTH), 0) * 16
    kk = jnp.where(kk >= 288, kk - 288, kk)
    spread = jnp.where((kk >= jj) & (kk < jj + 16), 1.0, 0.0).astype(jnp.bfloat16)

    def mask_of(ref):
        kept = jnp.where(ref[...] == 1, 1.0, 0.0).astype(jnp.bfloat16)
        kept = jnp.broadcast_to(kept, (16, 18))
        m = jnp.dot(kept, spread, preferred_element_type=jnp.float32)
        place = lax.broadcasted_iota(jnp.int32, (16, DEPTH), 1)
        return jnp.where(place < ROWS, m, 0.0).astype(jnp.bfloat16)

    def prepare(v, slot, first, mask):
        g = 2 * v + core
        tile = (224 * g) // 128 - g // 7
        off = 224 * g - 128 * tile
        window = fbuf[pl.ds(first, DEPTH), pl.ds(pl.multiple_of(tile * 128, 128), 384)]
        turned[slot] = window.T
        taken = turned[slot, pl.ds(pl.multiple_of(off, 32), 224), :] * mask[0:1]
        columns = pl.ds(first, DEPTH)
        g_rows[v, :, columns] = taken
        p_rows[v, :, columns] = jnp.dot(
            order[...], taken, preferred_element_type=jnp.float32
        ).astype(jnp.bfloat16)

    loads[4].wait()
    own_mask = mask_of(own_screen)
    own = fbuf[pl.ds(0, DEPTH), :]
    squares = jnp.dot(own_mask, own * own, preferred_element_type=jnp.float32)
    most = jnp.max(squares[0:8], axis=1, keepdims=True) * 1.02 + 1e-35
    sc_own[...] = jnp.broadcast_to(most, (8, 128))
    scale_swap = remote(sc_own, sc_peer, swap_send.at[8], swap_recv.at[8], peer)
    for i in range(4, 7):
        swap(i)
    for v in range(4):
        prepare(v, v, 0, own_mask)
    scale_swap.wait_recv()
    mine = sc_own[...] + sc_peer[...]
    mine_ref[...] = mine
    inverse = (1.0 / mine)[0:1, 0:1]
    scales1 = []
    for axis in range(3):
        for hop in HOPS:
            i = axis * 3 + hop - 1
            scales1.append(remote(mine_ref, sc1.at[i], ssend1.at[i], srecv1.at[i], along(axis, hop)))

    turns = [[(here[axes[1]] + hop) % 4 for hop in HOPS] + [here[axes[1]]] for axes, *_ in COLOURS]
    copies1 = {}

    def unit(c, j):
        _, col, cols = COLOURS[c]
        lhs = (g_rows if c == 0 else p_rows)[turns[c][j]]
        made = jnp.dot(lhs, fbuf[:, pl.ds(col, cols)], preferred_element_type=jnp.float32)
        whole[c][j][...] = made.reshape(4, 56, cols)

    def unit_by_place(hop):
        _, col, cols = COLOURS[1]
        lhs = g_rows[(here[Y] + hop) % 4]
        made = jnp.dot(lhs, fbuf[:, pl.ds(col, cols)], preferred_element_type=jnp.float32)
        whole[1][hop] = made.reshape(4, 56, cols)

    def emit(c, j):
        axis = COLOURS[c][0][0]
        for hop in HOPS:
            if c == 1:
                piece = whole[1][hop, turns[1][j]]
            else:
                piece = whole[c][j][(here[axis] + hop) % 4]
            q1[c][hop - 1, j] = coded(piece, inverse).astype(jnp.int16)
            copies1[c, j, hop] = remote(
                q1[c].at[hop - 1, j], r1[c].at[hop - 1, j], send1.at[c, hop - 1, j], recv1.at[c, hop - 1, j],
                along(axis, hop),
            )

    def first_sum(c, j):
        axis = COLOURS[c][0][0]
        total = whole[1][0, turns[1][j]] if c == 1 else whole[c][j][here[axis]]
        for hop in HOPS:
            copies1[c, j, hop].wait_recv()
            scale = sc1[axis * 3 + hop - 1][0:1, 0:1]
            total = total + decoded(r1[c][hop - 1, j], scale)
        return total

    def set_exponents():
        for copy in scales1:
            copy.wait_recv()
        for c, (axes, *_) in enumerate(COLOURS):
            i = axes[0] * 3
            bound = mine_ref[...] + sc1[i] + sc1[i + 1] + sc1[i + 2]
            exponents[c] = jnp.ceil(jnp.log(bound) * 1.4426950408889634 + 0.001)

    copies2 = {}

    def plane(c, j):
        axes, _, cols = COLOURS[c]
        total = first_sum(c, j)
        for w in range(4):
            b[c][j, w, 0:14, :] = total[w * 14 : w * 14 + 14]
        exponent = exponents[c][0:1, 0:1]
        inv = 1.0 / power(exponent)
        spare = exponent.astype(jnp.int32)
        row = lax.broadcasted_iota(jnp.int32, (16, cols), 0)
        hop2 = ALL[j]
        for k, hop3 in enumerate(ALL):
            if hop2 == 0 and hop3 == 0:
                continue
            w = (here[axes[2]] + hop3) % 4
            code = jnp.where(row < 14, coded(b[c][j, w], inv), spare)
            i = hop2 * 4 + hop3
            q2[c][i] = code.astype(jnp.int16)
            place = list(here)
            place[axes[1]] = turns[c][j]
            place[axes[2]] = w
            device = (place[Y] * 2 + core, place[X] * 4 + place[Z])
            copies2[c, i] = remote(q2[c].at[i], r2[c].at[i], send2.at[c, i], recv2.at[c, i], device)

    def last(c):
        axes, col, cols = COLOURS[c]
        total = b[c][3, here[axes[2]]]
        for hop2 in ALL:
            for hop3 in ALL:
                if hop2 == 0 and hop3 == 0:
                    continue
                i = hop2 * 4 + hop3
                copies2[c, i].wait_recv()
                code = r2[c][i].astype(jnp.int32)
                total = total + decoded(code, power(code[14:15].astype(jnp.float32)))
        o_ref[:, pl.ds(col, cols)] = total[0:14]

    landed = 0

    def land(upto):
        nonlocal landed
        while landed < upto:
            swaps[landed].wait_recv()
            landed += 1

    screen_swap.wait_recv()
    peer_mask = mask_of(peer_screen)
    land(7)
    along_y = turns[0]
    prepare(along_y[0], 0, DEPTH, peer_mask)
    unit(2, 0)
    emit(2, 0)
    unit(0, 0)
    emit(0, 0)
    prepare(along_y[1], 1, DEPTH, peer_mask)
    prepare(along_y[2], 2, DEPTH, peer_mask)
    unit_by_place(1)
    unit_by_place(3)
    unit_by_place(2)
    emit(1, 0)
    unit(2, 1)
    emit(1, 1)
    unit(0, 1)
    emit(2, 1)
    set_exponents()
    unit(2, 2)
    emit(0, 1)
    emit(1, 2)
    prepare(along_y[3], 3, DEPTH, peer_mask)
    unit(0, 2)
    emit(2, 2)
    emit(1, 3)
    unit(2, 3)
    emit(0, 2)
    unit(0, 3)
    emit(2, 3)
    unit_by_place(0)
    emit(0, 3)
    plane(0, 0)
    plane(1, 0)
    plane(2, 0)
    plane(0, 1)
    plane(1, 1)
    plane(2, 1)
    plane(1, 2)
    plane(0, 2)
    plane(2, 2)
    plane(1, 3)
    plane(0, 3)
    plane(2, 3)
    for copy in sent[:-45]:
        copy.wait_send()
    last(1)
    last(0)
    last(2)
    for copy in sent[-45:]:
        copy.wait_send()


def on_device(factors, screen):
    f32, i16, bf16 = jnp.float32, jnp.int16, jnp.bfloat16
    v = pltpu.VMEM
    dma = pltpu.SemaphoreType.DMA
    widths = [c[2] for c in COLOURS]

    def each(shape, dtype):
        return [v((*shape, w), dtype) for w in widths]

    scratch = [
        v((2 * DEPTH, NBF), bf16), v((4, 384, DEPTH), bf16), v((224, 224), bf16),
        v((4, 224, 2 * DEPTH), bf16), v((4, 224, 2 * DEPTH), bf16), *[v((4, 56, widths[0]), f32)] * 4,
        v((4, 4, 56, widths[1]), f32), *[v((4, 56, widths[2]), f32)] * 4,
        *each((3, 4, 56), i16), *each((3, 4, 56), i16),
        *each((16, 16), i16), *each((16, 16), i16), *each((4, 4, 16), f32),
        v((1, 18), jnp.int32), v((1, 18), jnp.int32), v((8, 128), f32), v((8, 128), f32), v((8, 128), f32),
        v((9, 8, 128), f32), v((3, 8, 128), f32),
        dma((5,)), dma((9,)), dma((9,)), dma((3, 3, 4)), dma((3, 3, 4)), dma((3, 16)), dma((3, 16)),
        dma((9,)), dma((9,)),
    ]
    return pl.pallas_call(
        kernel,
        out_shape=jax.ShapeDtypeStruct((14, NBF), f32),
        in_specs=[pl.BlockSpec(memory_space=pl.ANY)] * 2,
        out_specs=pl.BlockSpec(memory_space=pltpu.VMEM),
        scratch_shapes=scratch,
        compiler_params=pltpu.CompilerParams(
            collective_id=0, has_side_effects=True, vmem_limit_bytes=60 * 2**20
        ),
    )(factors.reshape(ROWS, NBF), screen)


def solution(mesh):
    placed = (P(("grp", "mem"), None, None), P(("grp", "mem"), None))
    return jax.shard_map(
        on_device, mesh=mesh, in_specs=placed, out_specs=P(("grp", "mem"), None), check_vma=False
    )
```

time: 202 us -> 40.8 us (0.20)
  waiting for transfers between devices: 111 us -> 0 us
  local copies, waits for them, and re-layouts: 43.4 us -> 1.55 us
  Pallas kernels: 0 us -> 39.1 us
  blocking collectives: 18.1 us -> 0 us
  between operations: 14.1 us -> 0.01 us
  matrix products: 9.72 us -> 0 us
  other arithmetic: 5.09 us -> 0 us
    unnamed x2 -> x0, waiting for transfers between devices: 111 us -> none
    pallas_call x0 -> x1, Pallas kernels: none -> 39.1 us  [on_device(): pl.pallas_call(kernel, out_shape=jax.ShapeDtypeStruct((14, NBF), f32), in...]
    reshape x3 -> x0, local copies, waits for them, and re-layouts: 35.6 us -> none  [the longest x2 33.7 us: on_device(): sectioned = whole.reshape(groups, members_all, own_rows, basis)]
    all_to_all x1 -> x0, blocking collectives: 18.1 us -> none  [sent_and_summed(): lax.all_to_all(blocks, axis, split_axis=0, concat_axis=0, tiled=True)]
    dot_general x1 -> x0, matrix products: 9.72 us -> none  [add_turn(): lax.dot_general(flat_rows, flat_rows, (((0,), (0,)), ((), ())), preferred...]
    broadcast_in_dim x1 -> x0, local copies, waits for them, and re-layouts: 5.51 us -> none  [on_device(): jnp.zeros((basis, basis), jnp.float32)]
    gather x1 -> x0, local copies, waits for them, and re-layouts: 2.25 us -> none  [add_turn(): chosen = jnp.take(blocks, picked, axis=1) * weight[None, :, None, None]]
  transfers between devices with their start and end apart: 1 -> 0, of which waited for: 1 -> 0; matrix products, arithmetic and copies ran while one was open for 0% -> 0% of each run, Pallas kernels for 0% -> 0%
where the time goes in v2:
time: 40.8 us; the launch traced here: 40.7 us
  Pallas kernels  39.1 us (96%)
  local copies, waits for them, and re-layouts  1.55 us (4%)
    pallas_call x1, Pallas kernels, on_device(): pl.pallas_call(kernel, out_shape=jax.ShapeDtypeStruct((14, NBF), f32), in...  39.1 us
    unnamed x1, local copies, waits for them, and re-layouts  1.55 us

profile of v2, /device:TPU:1, one launch (start us, length us, event | category | flops | bytes accessed | tf_op | source)
XLA Modules:
  0.0 40.7 jit_solution(7959466375418153710)
XLA Ops:
  0.0 39.1 %shard_map.28 = f32[14,1792]{1,0:T(8,128)} custom-call(bf16[576,1792]{1,0:T(8,128)(2,1)} %bitcast.1, s32[1,18]{1,0:T(1,128)} %s_ref.1), custom_call_target="tpu_custom_call" | custom-call | tf_op jit(solution)/shard_map/pallas_call | solution.py:319
  39.1 1.6 %copy.4 = f32[14,1792]{1,0:T(8,128)} copy(f32[14,1792]{1,0:T(8,128)} %shard_map.28) | data formatting | bytes 200704

commit v3 on v2

--- a/solution.py
+++ b/solution.py
@@ -319,11 +319,11 @@
     return pl.pallas_call(
         kernel,
         out_shape=jax.ShapeDtypeStruct((14, NBF), f32),
-        in_specs=[pl.BlockSpec(memory_space=pl.ANY)] * 2,
+        in_specs=[pl.BlockSpec(memory_space=pltpu.HBM)] * 2,
         out_specs=pl.BlockSpec(memory_space=pltpu.VMEM),
         scratch_shapes=scratch,
         compiler_params=pltpu.CompilerParams(
-            collective_id=0, has_side_effects=True, vmem_limit_bytes=60 * 2**20
+            collective_id=0, has_side_effects=True, vmem_limit_bytes=55000000
         ),
     )(factors.reshape(ROWS, NBF), screen)
 

time: 40.8 us -> 39.8 us (0.975)
  Pallas kernels: 39.1 us -> 38.3 us
    pallas_call x1, Pallas kernels: 39.1 us -> 38.3 us  [on_device(): pl.pallas_call(kernel, out_shape=jax.ShapeDtypeStruct((14, NBF), f32), in...]
    unnamed x1 -> x3, local copies, waits for them, and re-layouts: 1.55 us -> 1.3 us
where the time goes in v3:
time: 39.8 us; the launch traced here: 39.6 us
  Pallas kernels  38.3 us (96%)
  local copies, waits for them, and re-layouts  1.3 us (3%)
    pallas_call x1, Pallas kernels, on_device(): pl.pallas_call(kernel, out_shape=jax.ShapeDtypeStruct((14, NBF), f32), in...  38.3 us
    unnamed x3, local copies, waits for them, and re-layouts  1.3 us

profile of v3, /device:TPU:1, one launch (start us, length us, event | category | flops | bytes accessed | tf_op | source)
XLA Modules:
  0.0 39.6 jit_solution(4111294520449012938)
XLA Ops:
  0.0 0.0 copy-start
  0.0 0.7 %copy-done = s32[1,18]{1,0:T(1,128)S(1)} copy-done((s32[1,18]{1,0:T(1,128)S(1)}, s32[1,18]{1,0:T(1,128)}, u32[]{:S(2)}) %copy-start) | copy-done | bytes 96
  0.7 38.3 %shard_map.28 = f32[14,1792]{1,0:T(8,128)S(1)} custom-call(bf16[576,1792]{1,0:T(8,128)(2,1)} %bitcast.1, s32[1,18]{1,0:T(1,128)S(1)} %copy-done), custom_call_target="tpu_custom_call" | custom-call | tf_op jit(solution)/shard_map/pallas_call | solution.py:319
  39.0 0.6 %copy.4 = f32[14,1792]{1,0:T(8,128)} copy(f32[14,1792]{1,0:T(8,128)S(1)} %shard_map.28) | data formatting | bytes 200704
Async XLA Ops:
  0.0 0.7 %copy-start = (s32[1,18]{1,0:T(1,128)S(1)}, s32[1,18]{1,0:T(1,128)}, u32[]{:S(2)}) copy-start(s32[1,18]{1,0:T(1,128)} %s_ref.1) | copy-start | bytes 220

commit v4 on v3

--- a/solution.py
+++ b/solution.py
@@ -9,7 +9,7 @@
 NBF = 1792
 ROWS = 576
 DEPTH = 640
-CHUNK = 256
+CHUNK = 144
 TOP = 32000.0
 X, Y, Z = 0, 1, 2
 COLOURS = (((X, Y, Z), 0, 640), ((Y, X, Z), 1280, 512), ((Z, Y, X), 640, 640))
@@ -83,18 +83,16 @@
     swaps = []
 
     def swap(i):
-        columns = pl.ds(i * CHUNK, CHUNK)
         swaps.append(
             remote(
-                fbuf.at[pl.ds(0, ROWS), columns],
-                fbuf.at[pl.ds(DEPTH, ROWS), columns],
+                fbuf.at[pl.ds(i * CHUNK, CHUNK)], fbuf.at[pl.ds(DEPTH + i * CHUNK, CHUNK)],
                 swap_send.at[i], swap_recv.at[i], peer,
             )
         )
 
     for load in loads[:4]:
         load.wait()
-    for i in range(4):
+    for i in range(2):
         swap(i)
 
     r = lax.broadcasted_iota(jnp.int32, (224, 224), 0).astype(jnp.float32)
@@ -137,7 +135,7 @@
     most = jnp.max(squares[0:8], axis=1, keepdims=True) * 1.02 + 1e-35
     sc_own[...] = jnp.broadcast_to(most, (8, 128))
     scale_swap = remote(sc_own, sc_peer, swap_send.at[8], swap_recv.at[8], peer)
-    for i in range(4, 7):
+    for i in range(2, 4):
         swap(i)
     for v in range(4):
         prepare(v, v, 0, own_mask)
@@ -168,7 +166,7 @@
 
     def emit(c, j):
         axis = COLOURS[c][0][0]
-        for hop in HOPS:
+        for hop in (2, 1, 3):
             if c == 1:
                 piece = whole[1][hop, turns[1][j]]
             else:
@@ -208,7 +206,7 @@
         spare = exponent.astype(jnp.int32)
         row = lax.broadcasted_iota(jnp.int32, (16, cols), 0)
         hop2 = ALL[j]
-        for k, hop3 in enumerate(ALL):
+        for k, hop3 in enumerate((2, 1, 3, 0)):
             if hop2 == 0 and hop3 == 0:
                 continue
             w = (here[axes[2]] + hop3) % 4
@@ -244,7 +242,7 @@
 
     screen_swap.wait_recv()
     peer_mask = mask_of(peer_screen)
-    land(7)
+    land(4)
     along_y = turns[0]
     prepare(along_y[0], 0, DEPTH, peer_mask)
     unit(2, 0)
@@ -269,15 +267,15 @@
     unit(0, 2)
     emit(2, 2)
     emit(1, 3)
+    plane(2, 0)
     unit(2, 3)
     emit(0, 2)
+    plane(0, 0)
     unit(0, 3)
     emit(2, 3)
     unit_by_place(0)
     emit(0, 3)
-    plane(0, 0)
     plane(1, 0)
-    plane(2, 0)
     plane(0, 1)
     plane(1, 1)
     plane(2, 1)

time: 39.8 us -> 39.6 us (level)
  no operation moved by 1% of the time
where the time goes in v4:
time: 39.6 us; the launch traced here: 39.5 us
  Pallas kernels  38.2 us (96%)
  local copies, waits for them, and re-layouts  1.3 us (3%)
    pallas_call x1, Pallas kernels, on_device(): pl.pallas_call(kernel, out_shape=jax.ShapeDtypeStruct((14, NBF), f32), in...  38.2 us
    unnamed x3, local copies, waits for them, and re-layouts  1.3 us

profile of v4, /device:TPU:1, one launch (start us, length us, event | category | flops | bytes accessed | tf_op | source)
XLA Modules:
  0.0 39.5 jit_solution(13125619376873123540)
XLA Ops:
  0.0 0.0 copy-start
  0.0 0.7 %copy-done = s32[1,18]{1,0:T(1,128)S(1)} copy-done((s32[1,18]{1,0:T(1,128)S(1)}, s32[1,18]{1,0:T(1,128)}, u32[]{:S(2)}) %copy-start) | copy-done | bytes 96
  0.7 38.2 %shard_map.28 = f32[14,1792]{1,0:T(8,128)S(1)} custom-call(bf16[576,1792]{1,0:T(8,128)(2,1)} %bitcast.1, s32[1,18]{1,0:T(1,128)S(1)} %copy-done), custom_call_target="tpu_custom_call" | custom-call | tf_op jit(solution)/shard_map/pallas_call | solution.py:317
  38.9 0.6 %copy.4 = f32[14,1792]{1,0:T(8,128)} copy(f32[14,1792]{1,0:T(8,128)S(1)} %shard_map.28) | data formatting | bytes 200704
Async XLA Ops:
  0.0 0.7 %copy-start = (s32[1,18]{1,0:T(1,128)S(1)}, s32[1,18]{1,0:T(1,128)}, u32[]{:S(2)}) copy-start(s32[1,18]{1,0:T(1,128)} %s_ref.1) | copy-start | bytes 220

commit v5 on v4

--- a/solution.py
+++ b/solution.py
@@ -287,8 +287,8 @@
     plane(2, 3)
     for copy in sent[:-45]:
         copy.wait_send()
+    last(0)
     last(1)
-    last(0)
     last(2)
     for copy in sent[-45:]:
         copy.wait_send()

time: 39.6 us -> 39.6 us (level)
  no operation moved by 1% of the time
where the time goes in v5:
time: 39.6 us; the launch traced here: 39.5 us
  Pallas kernels  38.2 us (96%)
  local copies, waits for them, and re-layouts  1.3 us (3%)
    pallas_call x1, Pallas kernels, on_device(): pl.pallas_call(kernel, out_shape=jax.ShapeDtypeStruct((14, NBF), f32), in...  38.2 us
    unnamed x3, local copies, waits for them, and re-layouts  1.3 us

profile of v5, /device:TPU:1, one launch (start us, length us, event | category | flops | bytes accessed | tf_op | source)
XLA Modules:
  0.0 39.5 jit_solution(13300684531637040721)
XLA Ops:
  0.0 0.0 copy-start
  0.0 0.7 %copy-done = s32[1,18]{1,0:T(1,128)S(1)} copy-done((s32[1,18]{1,0:T(1,128)S(1)}, s32[1,18]{1,0:T(1,128)}, u32[]{:S(2)}) %copy-start) | copy-done | bytes 96
  0.7 38.2 %shard_map.28 = f32[14,1792]{1,0:T(8,128)S(1)} custom-call(bf16[576,1792]{1,0:T(8,128)(2,1)} %bitcast.1, s32[1,18]{1,0:T(1,128)S(1)} %copy-done), custom_call_target="tpu_custom_call" | custom-call | tf_op jit(solution)/shard_map/pallas_call | solution.py:317
  38.9 0.6 %copy.4 = f32[14,1792]{1,0:T(8,128)} copy(f32[14,1792]{1,0:T(8,128)S(1)} %shard_map.28) | data formatting | bytes 200704
Async XLA Ops:
  0.0 0.7 %copy-start = (s32[1,18]{1,0:T(1,128)S(1)}, s32[1,18]{1,0:T(1,128)}, u32[]{:S(2)}) copy-start(s32[1,18]{1,0:T(1,128)} %s_ref.1) | copy-start | bytes 220
